TPU v7x, 32 devices: a whole 2x2x4 slice. The times are simulated.
32 devices in a mesh: rows: 8 (over z, x), grp: 4 (over y, core).
Axes of the slice: x: 2, y: 2, z: 4, core: 2. Of those that a mesh axis runs over, the one named last changes fastest.
Arguments:
- user_features: bfloat16 [4, 2048, 256], P('grp', 'rows'), may hold values from -72 to 72
- w_first: bfloat16 [256, 256], replicated, may hold values from -0.375 to 0.375
- w_second: bfloat16 [256, 256], replicated, may hold values from -0.375 to 0.375
- item_embed: bfloat16 [4, 2048, 256], P('grp', 'rows'), may hold values from -27 to 27
- example_weight: float32 [4, 2048], P('grp', 'rows'), may hold values from 0.02 to 0.2
- positive: int32 [4, 2048], P('grp', 'rows'), may hold values from 0 to 2047
- item_owner: int32 [4, 2048, 1], P('grp', 'rows'), may hold values from 0 to 7; in each aligned block of 256 rows (0 to 255, 256 to 511, ..., all dimensions but the last counted through in order) at most 128 rows name the same one
- item_row: int32 [4, 2048], P('grp', 'rows'), may hold values from 0 to 4095
Outputs:
- grad_first: float32 [256, 256], replicated
- grad_second: float32 [256, 256], replicated
- grad_table: float32 [32768, 256], P('rows', 'grp')
Inputs may be any that keep to these rules, and one draw needn't show every extreme that they name: `item_owner`: within the rows of one device (aligned blocks of 256 pairs of a group) no owner is named by more than 128 pairs, a bound that some block reaches.
All inputs are finite; a program needn't handle non-finite values.
Results may differ from a plain program's by a relative error of at most 0.0023.
The roundings to bfloat16 on the way count: a program that leaves them out, or rounds other values in their place, can miss the bound.
Values may be sent and summed in bfloat16 or wider, within the bound.
A program may use at most 128 MiB of HBM per device.

v0:
```python
import jax
import jax.numpy as jnp
from jax import lax
from jax.sharding import PartitionSpec as P

ITEMS_DEV = 4096


def contract_first(left, right):
    return lax.dot_general(
        left, right, (((0,), (0,)), ((), ())), preferred_element_type=jnp.float32
    )


def contract_last(left, right):
    return lax.dot_general(
        left, right, (((1,), (1,)), ((), ())), preferred_element_type=jnp.float32
    )


def body(
    user_features, w_first, w_second, item_embed, example_weight, positive, item_owner, item_row
):
    features = user_features[0]
    own_items = item_embed[0]
    weights = example_weight[0]
    targets = positive[0]
    owners = item_owner[0, :, 0]
    item_rows = item_row[0]
    my_users = features.shape[0]
    feature_width = own_items.shape[1]
    peers = lax.axis_size("rows")
    my_index = lax.axis_index("rows")
    pre_act = jnp.dot(features, w_first, preferred_element_type=jnp.float32)
    hidden = jax.nn.silu(pre_act).astype(jnp.bfloat16)
    user_vecs = jnp.dot(hidden, w_second, preferred_element_type=jnp.float32).astype(jnp.bfloat16)
    gathered = lax.all_gather(own_items, "rows", axis=0, tiled=True)
    group_users = gathered.shape[0]
    scores = contract_last(user_vecs, gathered)
    row_max = jnp.max(scores, axis=1, keepdims=True)
    log_total = row_max + jnp.log(jnp.sum(jnp.exp(scores - row_max), axis=1, keepdims=True))
    columns = lax.broadcasted_iota(jnp.int32, (1, group_users), 1)
    chosen = (columns == targets[:, None]).astype(jnp.float32)
    dscore = (weights[:, None] * (jnp.exp(scores - log_total) - chosen)).astype(jnp.bfloat16)
    grad_user = jnp.dot(dscore, gathered, preferred_element_type=jnp.float32).astype(jnp.bfloat16)
    everyone = lax.all_gather(user_vecs, "rows", axis=0, tiled=True)
    target_all, total_all, weight_all = (
        lax.all_gather(targets.astype(jnp.float32), "rows", axis=0, tiled=True),
        lax.all_gather(log_total[:, 0], "rows", axis=0, tiled=True),
        lax.all_gather(weights, "rows", axis=0, tiled=True),
    )
    back_scores = contract_last(everyone, own_items)
    own_columns = my_index * my_users + lax.broadcasted_iota(jnp.int32, (1, my_users), 1)
    hits = (own_columns == target_all.astype(jnp.int32)[:, None]).astype(jnp.float32)
    back_dscore = (weight_all[:, None] * (jnp.exp(back_scores - total_all[:, None]) - hits)).astype(
        jnp.bfloat16
    )
    grad_item = contract_first(back_dscore, everyone)
    d_second = contract_first(hidden, grad_user)
    back_grad = contract_last(grad_user, w_second)
    sigmoid_pre = jax.nn.sigmoid(pre_act)
    grad_pre = (back_grad * sigmoid_pre * (1.0 + pre_act * (1.0 - sigmoid_pre))).astype(
        jnp.bfloat16
    )
    d_first = contract_first(features, grad_pre)
    grad_first, grad_second = lax.psum((d_first, d_second), ("rows", "grp"))
    capacity = max(2, 4 * my_users // peers)
    member = (owners[:, None] == lax.broadcasted_iota(jnp.int32, (1, peers), 1)).astype(jnp.int32)
    before = jnp.cumsum(member, axis=0) - member
    slot_rank = jnp.sum(before * member, axis=1)
    slots = owners * capacity + slot_rank
    send_grad = jnp.zeros((peers * capacity, feature_width), jnp.float32).at[slots].set(grad_item)
    send_grad = send_grad.reshape(peers, capacity, feature_width)
    send_rows = (
        jnp.full((peers * capacity,), -1.0, jnp.float32)
        .at[slots]
        .set(item_rows.astype(jnp.float32))
    )
    got_grad, got_rows = (
        lax.all_to_all(send_grad, "rows", split_axis=0, concat_axis=0, tiled=True),
        lax.all_to_all(
            send_rows.reshape(peers, capacity), "rows", split_axis=0, concat_axis=0, tiled=True
        ),
    )
    table_rows = got_rows.reshape(-1).astype(jnp.int32)
    table_rows = jnp.where(table_rows >= 0, table_rows, ITEMS_DEV)
    dense_grad = (
        jnp.zeros((ITEMS_DEV, feature_width), jnp.float32)
        .at[table_rows]
        .add(got_grad.reshape(-1, feature_width), mode="drop")
    )
    grad_table = lax.psum_scatter(dense_grad, "grp", scatter_dimension=1, tiled=True)
    return (grad_first, grad_second, grad_table)


def solution(mesh):
    placed = (
        P("grp", "rows", None),
        P(),
        P(),
        P("grp", "rows", None),
        P("grp", "rows"),
        P("grp", "rows"),
        P("grp", "rows", None),
        P("grp", "rows"),
    )
    return jax.shard_map(
        body, mesh=mesh, in_specs=placed, out_specs=(P(), P(), P("rows", "grp")), check_vma=False
    )
```

profile of v0, /device:TPU:0, one launch (start us, length us, event | category | flops | bytes accessed | tf_op | source)
XLA Modules:
  0.0 301.3 jit_solution(13880731240005856503)
XLA Ops:
  7.3 0.7 all-gather.9.cloned.1.call-update
  7.9 0.0 all-gather.7.cloned.1.call-start
  8.0 1.2 fusion.27
  9.2 0.9 convolution_convert_fusion
  10.1 0.7 convert_element_type.64
  10.7 0.6 reduce-window.6
  11.3 0.2 slice_reduce_fusion
  11.6 0.1 fusion.31
  11.7 2.0 scatter_custom_fusion
  13.7 7.3 %all-to-all-start = ((f32[8,1,128]{2,1,0:T(1,128)}), f32[8,1,128]{2,1,0:T(1,128)S(1)}, u32[]{:S(2)}, u32[]{:S(2)}) async-start(f32[8,1,128]{2,1,0:T(1,128)} %bitcast.13), calls=%async_computation | async-start | bytes 8192 | tf_op jit(solution)/shard_map/all_to_all | solution.py:81
  21.0 21.1 %all-gather.3 = f32[8,1,256]{2,1,0:T(1,128)S(1)} all-gather(f32[1,1,256]{2,1,0:T(1,128)S(1)} %bitcast.67), channel_id=1, replica_groups=mesh['rows'=8,'grp'=4] {'rows'}, dimensions={0}, use_global_device_ids=true | all-gather | bytes 9216 | tf_op jit(solution)/shard_map/all_gather | solution.py:48
  42.1 16.3 %all-gather.1 = f32[1,2048]{1,0:T(1,128)S(1)} all-gather(f32[1,256]{1,0:T(1,128)S(1)} %copy-done.4), channel_id=3, replica_groups=mesh['rows'=8,'grp'=4] {'rows'}, dimensions={1}, use_global_device_ids=true | all-gather | bytes 9216 | tf_op jit(solution)/shard_map/all_gather | solution.py:50
  58.4 1.9 fusion.37
  60.3 0.4 exponential_reduce_fusion
  60.7 18.3 %all-gather.2 = f32[8,1,256]{2,1,0:T(1,128)S(1)} all-gather(f32[1,1,256]{2,1,0:T(1,128)S(1)} %bitcast.66), channel_id=1, replica_groups=mesh['rows'=8,'grp'=4] {'rows'}, dimensions={0}, use_global_device_ids=true | all-gather | bytes 9216 | tf_op jit(solution)/shard_map/all_gather | solution.py:49
  79.1 16.1 %all-gather.7.cloned.1.call-done = bf16[2048,256]{1,0:T(8,128)(2,1)} async-done(((bf16[256,256]{1,0:T(8,128)(2,1)}), bf16[2048,256]{1,0:T(8,128)(2,1)}) %all-gather.7.cloned.1.call-update) | async-done | bytes 1048592 | tf_op jit(solution)/shard_map/all_gather | solution.py:46
  95.2 3.9 %fusion.6 = f32[256,256]{1,0:T(8,128)} fusion(bf16[2048,256]{1,0:T(8,128)(2,1)} %all-gather.7.cloned.1.call-done, s32[256]{0:T(256)S(1)} %iota_add_fusion, f32[2048]{0:T(1024)S(1)} %bitcast.64, f32[2048]{0:T(1024)S(1)} %bitcast.63, s32[2048]{0:T(1024)S(1)} %bitcast.65, bf16[1,256,256]{2,1,0:T(8,128)(2,1)S(1)} %copy-done.2), kind=kOutput, calls=%fused_computation.13 | convolution fusion | flops 540016640 | bytes 1467392 | tf_op jit(solution)/shard_map/dot_general | solution.py:10
  99.1 2.9 scatter_custom_fusion.1
  102.0 4.4 %all-to-all-start.1 = ((f32[8,128,256]{2,1,0:T(8,128)}), f32[8,128,256]{2,1,0:T(8,128)}, u32[]{:S(2)}, u32[]{:S(2)}) async-start(f32[8,128,256]{2,1,0:T(8,128)} %bitcast.22), calls=%async_computation.1 | async-start | bytes 2097152 | tf_op jit(solution)/shard_map/all_to_all | solution.py:80
  106.3 0.0 all-reduce.3.cloned.1.call-start
  106.4 0.8 convolution_convert_fusion.1
  107.2 0.6 copy-done.7
  107.8 1.0 fusion.36
  108.8 2.1 convolution_bitcast_fusion
  111.0 0.0 reduce-scatter.4.cloned.1.call-start
  111.0 20.8 %all-to-all-done.1 = f32[8,128,256]{2,1,0:T(8,128)} async-done(((f32[8,128,256]{2,1,0:T(8,128)}), f32[8,128,256]{2,1,0:T(8,128)}, u32[]{:S(2)}, u32[]{:S(2)}) %all-to-all-start.1) | async-done | bytes 1048608 | tf_op jit(solution)/shard_map/all_to_all | solution.py:80
  131.8 8.7 %scatter_custom_fusion.2 = f32[4096,256]{1,0:T(8,128)} fusion(s32[1024]{0:T(1024)S(1)} %bitcast.68, f32[1024,256]{1,0:T(8,128)} %bitcast.23, f32[]{:T(128)} %constant.13.clone.1), kind=kCustom, calls=%fused_computation.8 | custom fusion | flops 262144 | bytes 4194816 | tf_op jit(solution)/shard_map/scatter-add | solution.py:90
  140.5 5.7 %copy.16 = f32[4096,256]{0,1:T(8,128)} copy(f32[4096,256]{1,0:T(8,128)} %scatter_custom_fusion.2) | data formatting | bytes 8388608
  146.2 100.4 %all-reduce.3.cloned.1.call-done = (f32[256,256]{0,1:T(8,128)}, f32[256,256]{1,0:T(8,128)}) async-done(((f32[256,256]{0,1:T(8,128)}, f32[256,256]{1,0:T(8,128)}), (f32[256,256]{0,1:T(8,128)}, f32[256,256]{1,0:T(8,128)})) %all-reduce.3.cloned.1.call-update) | async-done | bytes 524304 | tf_op jit(solution)/shard_map/psum | solution.py:66
  246.5 1.8 copy.14
  248.3 44.8 %reduce-scatter.4.cloned.1.call-done = f32[64,4096]{1,0:T(8,128)} async-done(((f32[256,4096]{1,0:T(8,128)}), f32[64,4096]{1,0:T(8,128)}) %reduce-scatter.4.cloned.1.call-update) | async-done | bytes 1048592
  293.1 1.7 copy.20
  (30 shorter events, 0.2 us)
Async XLA Ops:
  7.2 2.0 copy-start
  7.2 3.6 %copy-start.3 = (s32[1,256,1]{1,2,0:T(1,128)S(1)}, s32[1,256,1]{1,2,0:T(1,128)}, u32[]{:S(2)}) copy-start(s32[1,256,1]{1,2,0:T(1,128)} %param.14) | copy-start | bytes 3076
  7.2 13.8 %copy-start.5 = (s32[1,256]{1,0:T(1,128)S(1)}, s32[1,256]{1,0:T(1,128)}, u32[]{:S(2)}) copy-start(s32[1,256]{1,0:T(1,128)} %param.13) | copy-start | bytes 3076
  7.2 34.9 %copy-start.4 = (f32[1,256]{1,0:T(1,128)S(1)}, f32[1,256]{1,0:T(1,128)}, u32[]{:S(2)}) copy-start(f32[1,256]{1,0:T(1,128)} %param.12) | copy-start | bytes 3076
  7.2 51.2 %all-gather.9.cloned.1.call-start = ((), (), s32[]{:S(2)}) async-start(), calls=%async_computation.4 | async-start | bytes 1179648 | tf_op jit(solution)/shard_map/all_gather | solution.py:37
  7.9 87.2 %all-gather.7.cloned.1.call-start = ((), (), s32[]{:S(2)}) async-start(), calls=%async_computation.3 | async-start | bytes 1179648 | tf_op jit(solution)/shard_map/all_gather | solution.py:46
  13.7 88.3 %all-to-all-start = ((f32[8,1,128]{2,1,0:T(1,128)}), f32[8,1,128]{2,1,0:T(1,128)S(1)}, u32[]{:S(2)}, u32[]{:S(2)}) async-start(f32[8,1,128]{2,1,0:T(1,128)} %bitcast.13), calls=%async_computation | async-start | bytes 8192 | tf_op jit(solution)/shard_map/all_to_all | solution.py:81
  58.4 36.8 %copy-start.2 = (bf16[1,256,256]{2,1,0:T(8,128)(2,1)S(1)}, bf16[1,256,256]{2,1,0:T(8,128)(2,1)}, u32[]{:S(2)}) copy-start(bf16[1,256,256]{2,1,0:T(8,128)(2,1)} %param.11) | copy-start | bytes 393220
  99.1 7.3 %copy-start.1 = (bf16[1,2048,256]{2,1,0:T(8,128)(2,1)S(1)}, bf16[1,2048,256]{2,1,0:T(8,128)(2,1)}, u32[]{:S(2)}) copy-start(bf16[1,2048,256]{2,1,0:T(8,128)(2,1)} %all-gather.9.cloned.1.call-done) | copy-start | bytes 3145732
  102.0 4.4 %copy-start.6 = (s32[1,256]{1,0:T(1,128)S(1)}, s32[1,256]{1,0:T(1,128)}, u32[]{:S(2)}) copy-start(s32[1,256]{1,0:T(1,128)} %param.13) | copy-start | bytes 3076
  102.0 29.8 %all-to-all-start.1 = ((f32[8,128,256]{2,1,0:T(8,128)}), f32[8,128,256]{2,1,0:T(8,128)}, u32[]{:S(2)}, u32[]{:S(2)}) async-start(f32[8,128,256]{2,1,0:T(8,128)} %bitcast.22), calls=%async_computation.1 | async-start | bytes 2097152 | tf_op jit(solution)/shard_map/all_to_all | solution.py:80
  106.3 140.2 %all-reduce.3.cloned.1.call-start = ((), (), s32[]{:S(2)}) async-start(), calls=%async_computation.6 | async-start | bytes 1048576 | tf_op jit(solution)/shard_map/psum | solution.py:66
  107.2 0.6 copy-start.7
  111.0 182.1 %reduce-scatter.4.cloned.1.call-start = ((), (), s32[]{:S(2)}) async-start(), calls=%async_computation.5 | async-start | bytes 5242880
Sparse Core Ops, SparseCore 0:
  10.1 43.2 all-gather.8
  56.1 38.9 all-gather.6
  113.2 133.2 all-reduce.2
  249.5 43.5 reduce-scatter.3
where the time goes:
time: 302 us; the launch traced here: 301 us
  waiting for transfers between devices  183 us (61%)
  blocking collectives  55.7 us (18%)
  local copies, waits for them, and re-layouts  14.9 us (5%)
  between operations  13.9 us (5%)
  starting transfers between devices  11.8 us (4%)
  matrix products  11.7 us (4%)
  other arithmetic  10.6 us (4%)
    psum x1, waiting for transfers between devices, body(): grad_first, grad_second = lax.psum((d_first, d_second), ('rows', 'grp'))  100 us
    unnamed x5, waiting for transfers between devices  45.5 us
    all_gather x1, blocking collectives, body(): lax.all_gather(targets.astype(jnp.float32), 'rows', axis=0, tiled=True)  21.1 us
    all_to_all x1, waiting for transfers between devices, body(): lax.all_to_all(send_grad, 'rows', split_axis=0, concat_axis=0, tiled=True)  20.8 us
    all_gather x1, blocking collectives, body(): lax.all_gather(log_total[:, 0], 'rows', axis=0, tiled=True)  18.3 us
    all_gather x1, blocking collectives, body(): lax.all_gather(weights, 'rows', axis=0, tiled=True)  16.3 us
    all_gather x1, waiting for transfers between devices, body(): everyone = lax.all_gather(user_vecs, 'rows', axis=0, tiled=True)  16.1 us
    unnamed x19, local copies, waits for them, and re-layouts  9.79 us
  transfers between devices with their start and end apart: 6, of which 4 were waited for; matrix products, arithmetic and copies ran while one was open for 12% of the time, Pallas kernels for 0%

commit v1 on v0

--- a/solution.py
+++ b/solution.py
@@ -43,7 +43,12 @@
     chosen = (columns == targets[:, None]).astype(jnp.float32)
     dscore = (weights[:, None] * (jnp.exp(scores - log_total) - chosen)).astype(jnp.bfloat16)
     grad_user = jnp.dot(dscore, gathered, preferred_element_type=jnp.float32).astype(jnp.bfloat16)
-    everyone = lax.all_gather(user_vecs, "rows", axis=0, tiled=True)
+    ring = [user_vecs]
+    for hop in range(7):
+        ring.append(lax.ppermute(ring[-1], "rows", [(dev, (dev + 1) % 8) for dev in range(8)]))
+    everyone = jnp.roll(
+        jnp.concatenate(ring[::-1], axis=0), (lax.axis_index("rows") + 1) * ring[0].shape[0], axis=0
+    )
     target_all, total_all, weight_all = (
         lax.all_gather(targets.astype(jnp.float32), "rows", axis=0, tiled=True),
         lax.all_gather(log_total[:, 0], "rows", axis=0, tiled=True),

time: 302 us -> 341 us (1.13)
  waiting for transfers between devices: 183 us -> 207 us
  local copies, waits for them, and re-layouts: 14.9 us -> 25.3 us
    ppermute x0 -> x7, waiting for transfers between devices: none -> 44.1 us  [body(): lax.ppermute(ring[-1], 'rows', [(dev, (dev + 1) % 8) for dev in range(8)])]
    all_gather x1 -> x0, waiting for transfers between devices: 16.1 us -> none  [body(): everyone = lax.all_gather(user_vecs, 'rows', axis=0, tiled=True)]
    unnamed x19 -> x36, local copies, waits for them, and re-layouts: 9.79 us -> 19.6 us
    all_to_all x1, waiting for transfers between devices: 20.8 us -> 11.7 us  [body(): lax.all_to_all(send_grad, 'rows', split_axis=0, concat_axis=0, tiled=True)]
    psum x1, waiting for transfers between devices: 100 us -> 107 us  [body(): grad_first, grad_second = lax.psum((d_first, d_second), ('rows', 'grp'))]
    unnamed x5 -> x4, waiting for transfers between devices: 45.5 us -> 45 us
  transfers between devices with their start and end apart: 6 -> 12, of which waited for: 4 -> 9; matrix products, arithmetic and copies ran while one was open for 12% -> 13% of each run, Pallas kernels for 0% -> 0%
where the time goes in v1:
time: 341 us; the launch traced here: 340 us
  waiting for transfers between devices  207 us (61%)
  blocking collectives  55.7 us (16%)
  local copies, waits for them, and re-layouts  25.3 us (7%)
  between operations  13.9 us (4%)
  starting transfers between devices  13.4 us (4%)
  other arithmetic  13.3 us (4%)
  matrix products  10.9 us (3%)
    psum x1, waiting for transfers between devices, body(): grad_first, grad_second = lax.psum((d_first, d_second), ('rows', 'grp'))  107 us
    unnamed x4, waiting for transfers between devices  45 us
    ppermute x7, waiting for transfers between devices, body(): lax.ppermute(ring[-1], 'rows', [(dev, (dev + 1) % 8) for dev in range(8)])  44.1 us
    all_gather x1, blocking collectives, body(): lax.all_gather(targets.astype(jnp.float32), 'rows', axis=0, tiled=True)  21.1 us
    unnamed x36, local copies, waits for them, and re-layouts  19.6 us
    all_gather x1, blocking collectives, body(): lax.all_gather(log_total[:, 0], 'rows', axis=0, tiled=True)  18.4 us
    all_gather x1, blocking collectives, body(): lax.all_gather(weights, 'rows', axis=0, tiled=True)  16.3 us
    all_to_all x1, waiting for transfers between devices, body(): lax.all_to_all(send_grad, 'rows', split_axis=0, concat_axis=0, tiled=True)  11.7 us
  transfers between devices with their start and end apart: 12, of which 9 were waited for; matrix products, arithmetic and copies ran while one was open for 13% of the time, Pallas kernels for 0%

profile of v1, /device:TPU:0, one launch (start us, length us, event | category | flops | bytes accessed | tf_op | source)
XLA Modules:
  0.0 340.0 jit_solution(9813257068530009780)
XLA Ops:
  7.2 1.2 fusion.29
  8.6 3.0 collective-permute-start
  11.7 6.5 %collective-permute-done = bf16[256,256]{1,0:T(8,128)(2,1)S(1)} collective-permute-done((bf16[256,256]{1,0:T(8,128)(2,1)S(1)}, bf16[256,256]{1,0:T(8,128)(2,1)S(1)}, u32[]{:S(2)}, u32[]{:S(2)}) %collective-permute-start) | collective-permute-done | bytes 131104 | tf_op jit(solution)/shard_map/ppermute | solution.py:48
  18.2 7.7 %collective-permute-done.1 = bf16[256,256]{1,0:T(8,128)(2,1)S(1)} collective-permute-done((bf16[256,256]{1,0:T(8,128)(2,1)S(1)}, bf16[256,256]{1,0:T(8,128)(2,1)S(1)}, u32[]{:S(2)}, u32[]{:S(2)}) %collective-permute-start.1) | collective-permute-done | bytes 131104 | tf_op jit(solution)/shard_map/ppermute | solution.py:48
  25.9 7.7 %collective-permute-done.2 = bf16[256,256]{1,0:T(8,128)(2,1)S(1)} collective-permute-done((bf16[256,256]{1,0:T(8,128)(2,1)S(1)}, bf16[256,256]{1,0:T(8,128)(2,1)S(1)}, u32[]{:S(2)}, u32[]{:S(2)}) %collective-permute-start.2) | collective-permute-done | bytes 131104 | tf_op jit(solution)/shard_map/ppermute | solution.py:48
  33.6 7.6 %collective-permute-done.3 = bf16[256,256]{1,0:T(8,128)(2,1)S(1)} collective-permute-done((bf16[256,256]{1,0:T(8,128)(2,1)S(1)}, bf16[256,256]{1,0:T(8,128)(2,1)S(1)}, u32[]{:S(2)}, u32[]{:S(2)}) %collective-permute-start.3) | collective-permute-done | bytes 131104 | tf_op jit(solution)/shard_map/ppermute | solution.py:48
  41.2 0.7 fusion.34
  42.4 7.2 %collective-permute-done.4 = bf16[256,256]{1,0:T(8,128)(2,1)S(1)} collective-permute-done((bf16[256,256]{1,0:T(8,128)(2,1)S(1)}, bf16[256,256]{1,0:T(8,128)(2,1)S(1)}, u32[]{:S(2)}, u32[]{:S(2)}) %collective-permute-start.4) | collective-permute-done | bytes 131104 | tf_op jit(solution)/shard_map/ppermute | solution.py:48
  49.9 0.8 fusion.33
  50.7 7.4 %collective-permute-done.5 = bf16[256,256]{1,0:T(8,128)(2,1)S(1)} collective-permute-done((bf16[256,256]{1,0:T(8,128)(2,1)S(1)}, bf16[256,256]{1,0:T(8,128)(2,1)S(1)}, u32[]{:S(2)}, u32[]{:S(2)}) %collective-permute-start.5) | collective-permute-done | bytes 131104 | tf_op jit(solution)/shard_map/ppermute | solution.py:48
  58.1 0.7 compare_select_fusion.2
  58.8 0.7 convert_element_type.64
  59.5 2.0 scatter_custom_fusion
  61.4 6.0 %all-to-all-start = ((f32[8,1,128]{2,1,0:T(1,128)}), f32[8,1,128]{2,1,0:T(1,128)S(1)}, u32[]{:S(2)}, u32[]{:S(2)}) async-start(f32[8,1,128]{2,1,0:T(1,128)} %bitcast.13), calls=%async_computation | async-start | bytes 8192 | tf_op jit(solution)/shard_map/all_to_all | solution.py:86
  67.4 0.7 convert_element_type.68
  68.1 21.1 %all-gather.3 = f32[8,1,256]{2,1,0:T(1,128)S(1)} all-gather(f32[1,1,256]{2,1,0:T(1,128)S(1)} %bitcast.65), channel_id=1, replica_groups=mesh['rows'=8,'grp'=4] {'rows'}, dimensions={0}, use_global_device_ids=true | all-gather | bytes 9216 | tf_op jit(solution)/shard_map/all_gather | solution.py:53
  89.2 16.3 %all-gather.1 = f32[1,2048]{1,0:T(1,128)S(1)} all-gather(f32[1,256]{1,0:T(1,128)S(1)} %copy-done.6), channel_id=3, replica_groups=mesh['rows'=8,'grp'=4] {'rows'}, dimensions={1}, use_global_device_ids=true | all-gather | bytes 9216 | tf_op jit(solution)/shard_map/all_gather | solution.py:55
  116.0 1.8 fusion.41
  118.3 18.4 %all-gather.2 = f32[8,1,256]{2,1,0:T(1,128)S(1)} all-gather(f32[1,1,256]{2,1,0:T(1,128)S(1)} %bitcast.64), channel_id=1, replica_groups=mesh['rows'=8,'grp'=4] {'rows'}, dimensions={0}, use_global_device_ids=true | all-gather | bytes 9216 | tf_op jit(solution)/shard_map/all_gather | solution.py:54
  136.7 3.8 %fusion.6 = f32[256,256]{1,0:T(8,128)} fusion(s32[256]{0:T(256)S(1)} %iota_add_fusion, f32[2048]{0:T(1024)S(1)} %bitcast.62, bf16[4096,256]{1,0:T(8,128)(2,1)} %constant_dynamic-update-slice_fusion, s32[]{:T(128)S(6)} %select_n.49, f32[2048]{0:T(1024)S(1)} %bitcast.61, s32[2048]{0:T(1024)S(1)} %bitcast.63, bf16[1,256,256]{2,1,0:T(8,128)(2,1)S(1)} %copy-done.4), kind=kOutput, calls=%fused_computation.13 | convolution fusion | flops 540016640 | bytes 2516992 | tf_op jit(solution)/shard_map/dot_general | solution.py:10
  140.5 2.9 scatter_custom_fusion.1
  143.4 4.2 %all-to-all-start.1 = ((f32[8,128,256]{2,1,0:T(8,128)}), f32[8,128,256]{2,1,0:T(8,128)}, u32[]{:S(2)}, u32[]{:S(2)}) async-start(f32[8,128,256]{2,1,0:T(8,128)} %bitcast.22), calls=%async_computation.1 | async-start | bytes 2097152 | tf_op jit(solution)/shard_map/all_to_all | solution.py:85
  147.7 0.8 convolution_convert_fusion.1
  149.1 1.0 fusion.40
  150.1 2.2 convolution_bitcast_fusion
  152.4 11.7 %all-to-all-done.1 = f32[8,128,256]{2,1,0:T(8,128)} async-done(((f32[8,128,256]{2,1,0:T(8,128)}), f32[8,128,256]{2,1,0:T(8,128)}, u32[]{:S(2)}, u32[]{:S(2)}) %all-to-all-start.1) | async-done | bytes 1048608 | tf_op jit(solution)/shard_map/all_to_all | solution.py:85
  164.1 8.7 %scatter_custom_fusion.2 = f32[4096,256]{1,0:T(8,128)} fusion(s32[1024]{0:T(1024)S(1)} %bitcast.66, f32[1024,256]{1,0:T(8,128)} %bitcast.23, f32[]{:T(128)} %constant.22.clone.1), kind=kCustom, calls=%fused_computation.8 | custom fusion | flops 262144 | bytes 4194816 | tf_op jit(solution)/shard_map/scatter-add | solution.py:95
  172.8 5.6 %copy.16 = f32[4096,256]{0,1:T(8,128)} copy(f32[4096,256]{1,0:T(8,128)} %scatter_custom_fusion.2) | data formatting | bytes 8388608
  178.4 106.7 %all-reduce.3.cloned.1.call-done = (f32[256,256]{0,1:T(8,128)}, f32[256,256]{1,0:T(8,128)}) async-done(((f32[256,256]{0,1:T(8,128)}, f32[256,256]{1,0:T(8,128)}), (f32[256,256]{0,1:T(8,128)}, f32[256,256]{1,0:T(8,128)})) %all-reduce.3.cloned.1.call-update) | async-done | bytes 524304 | tf_op jit(solution)/shard_map/psum | solution.py:71
  285.1 1.8 copy.14
  286.9 44.9 %reduce-scatter.4.cloned.1.call-done = f32[64,4096]{1,0:T(8,128)} async-done(((f32[256,4096]{1,0:T(8,128)}), f32[64,4096]{1,0:T(8,128)}) %reduce-scatter.4.cloned.1.call-update) | async-done | bytes 1048592
  331.8 1.7 copy.35
  (59 shorter events, 12.9 us)
Async XLA Ops:
  7.2 1.2 copy-start
  7.2 82.0 %copy-start.6 = (f32[1,256]{1,0:T(1,128)S(1)}, f32[1,256]{1,0:T(1,128)}, u32[]{:S(2)}) copy-start(f32[1,256]{1,0:T(1,128)} %param.12) | copy-start | bytes 3076
  7.2 108.8 %all-gather.6.cloned.1.call-start = ((), (), s32[]{:S(2)}) async-start(), calls=%async_computation.3 | async-start | bytes 1179648 | tf_op jit(solution)/shard_map/all_gather | solution.py:37
  8.4 25.1 %copy-start.2 = (f32[256,256]{1,0:T(8,128)}, f32[256,256]{1,0:T(8,128)S(1)}, u32[]{:S(2)}) copy-start(f32[256,256]{1,0:T(8,128)S(1)} %fusion.29) | copy-start | bytes 786436
  8.6 9.6 %collective-permute-start = (bf16[256,256]{1,0:T(8,128)(2,1)S(1)}, bf16[256,256]{1,0:T(8,128)(2,1)S(1)}, u32[]{:S(2)}, u32[]{:S(2)}) collective-permute-start(bf16[256,256]{1,0:T(8,128)(2,1)S(1)} %convolution_convert_fusion), channel_id=1, source_target_pairs={{0,4},{4,8},{8,12},{12,16},{16,20},{20,24},{24,28},{28,0},{1,5},{5... | collective-permute-start | bytes 393224 | tf_op jit(solution)/shard_map/ppermute | solution.py:48
  18.2 7.7 %collective-permute-start.1 = (bf16[256,256]{1,0:T(8,128)(2,1)S(1)}, bf16[256,256]{1,0:T(8,128)(2,1)S(1)}, u32[]{:S(2)}, u32[]{:S(2)}) collective-permute-start(bf16[256,256]{1,0:T(8,128)(2,1)S(1)} %collective-permute-done), channel_id=1, source_target_pairs={{0,4},{4,8},{8,12},{12,16},{16,20},{20,24},{24,28},{28,0},{1,5},{5... | collective-permute-start | bytes 393224 | tf_op jit(solution)/shard_map/ppermute | solution.py:48
  25.9 7.7 %collective-permute-start.2 = (bf16[256,256]{1,0:T(8,128)(2,1)S(1)}, bf16[256,256]{1,0:T(8,128)(2,1)S(1)}, u32[]{:S(2)}, u32[]{:S(2)}) collective-permute-start(bf16[256,256]{1,0:T(8,128)(2,1)S(1)} %collective-permute-done.1), channel_id=1, source_target_pairs={{0,4},{4,8},{8,12},{12,16},{16,20},{20,24},{24,28},{28,0},{1,5},{5... | collective-permute-start | bytes 393224 | tf_op jit(solution)/shard_map/ppermute | solution.py:48
  33.5 7.7 %collective-permute-start.3 = (bf16[256,256]{1,0:T(8,128)(2,1)S(1)}, bf16[256,256]{1,0:T(8,128)(2,1)S(1)}, u32[]{:S(2)}, u32[]{:S(2)}) collective-permute-start(bf16[256,256]{1,0:T(8,128)(2,1)S(1)} %collective-permute-done.2), channel_id=1, source_target_pairs={{0,4},{4,8},{8,12},{12,16},{16,20},{20,24},{24,28},{28,0},{1,5},{5... | collective-permute-start | bytes 393224 | tf_op jit(solution)/shard_map/ppermute | solution.py:48
  41.2 8.5 %collective-permute-start.4 = (bf16[256,256]{1,0:T(8,128)(2,1)S(1)}, bf16[256,256]{1,0:T(8,128)(2,1)S(1)}, u32[]{:S(2)}, u32[]{:S(2)}) collective-permute-start(bf16[256,256]{1,0:T(8,128)(2,1)S(1)} %collective-permute-done.3), channel_id=1, source_target_pairs={{0,4},{4,8},{8,12},{12,16},{16,20},{20,24},{24,28},{28,0},{1,5},{5... | collective-permute-start | bytes 393224 | tf_op jit(solution)/shard_map/ppermute | solution.py:48
  49.6 8.5 %collective-permute-start.5 = (bf16[256,256]{1,0:T(8,128)(2,1)S(1)}, bf16[256,256]{1,0:T(8,128)(2,1)S(1)}, u32[]{:S(2)}, u32[]{:S(2)}) collective-permute-start(bf16[256,256]{1,0:T(8,128)(2,1)S(1)} %collective-permute-done.4), channel_id=1, source_target_pairs={{0,4},{4,8},{8,12},{12,16},{16,20},{20,24},{24,28},{28,0},{1,5},{5... | collective-permute-start | bytes 393224 | tf_op jit(solution)/shard_map/ppermute | solution.py:48
  58.1 47.4 %collective-permute-start.6 = (bf16[256,256]{1,0:T(8,128)(2,1)S(1)}, bf16[256,256]{1,0:T(8,128)(2,1)S(1)}, u32[]{:S(2)}, u32[]{:S(2)}) collective-permute-start(bf16[256,256]{1,0:T(8,128)(2,1)S(1)} %collective-permute-done.5), channel_id=1, source_target_pairs={{0,4},{4,8},{8,12},{12,16},{16,20},{20,24},{24,28},{28,0},{1,5},{5... | collective-permute-start | bytes 393224 | tf_op jit(solution)/shard_map/ppermute | solution.py:48
  61.4 81.9 %all-to-all-start = ((f32[8,1,128]{2,1,0:T(1,128)}), f32[8,1,128]{2,1,0:T(1,128)S(1)}, u32[]{:S(2)}, u32[]{:S(2)}) async-start(f32[8,1,128]{2,1,0:T(1,128)} %bitcast.13), calls=%async_computation | async-start | bytes 8192 | tf_op jit(solution)/shard_map/all_to_all | solution.py:86
  116.0 20.6 %copy-start.4 = (bf16[1,256,256]{2,1,0:T(8,128)(2,1)S(1)}, bf16[1,256,256]{2,1,0:T(8,128)(2,1)}, u32[]{:S(2)}) copy-start(bf16[1,256,256]{2,1,0:T(8,128)(2,1)} %param.11) | copy-start | bytes 393220
  140.5 7.2 %copy-start.1 = (bf16[1,2048,256]{2,1,0:T(8,128)(2,1)S(1)}, bf16[1,2048,256]{2,1,0:T(8,128)(2,1)}, u32[]{:S(2)}) copy-start(bf16[1,2048,256]{2,1,0:T(8,128)(2,1)} %all-gather.6.cloned.1.call-done) | copy-start | bytes 3145732
  140.5 7.2 %copy-start.7 = (s32[1,256]{1,0:T(1,128)S(1)}, s32[1,256]{1,0:T(1,128)}, u32[]{:S(2)}) copy-start(s32[1,256]{1,0:T(1,128)} %param.13) | copy-start | bytes 3076
  143.4 20.7 %all-to-all-start.1 = ((f32[8,128,256]{2,1,0:T(8,128)}), f32[8,128,256]{2,1,0:T(8,128)}, u32[]{:S(2)}, u32[]{:S(2)}) async-start(f32[8,128,256]{2,1,0:T(8,128)} %bitcast.22), calls=%async_computation.1 | async-start | bytes 2097152 | tf_op jit(solution)/shard_map/all_to_all | solution.py:85
  147.6 137.5 %all-reduce.3.cloned.1.call-start = ((), (), s32[]{:S(2)}) async-start(), calls=%async_computation.5 | async-start | bytes 1048576 | tf_op jit(solution)/shard_map/psum | solution.py:71
  147.7 1.4 copy-start.3
  147.7 2.4 copy-start.5
  148.5 0.6 copy-start.8
  152.3 179.5 %reduce-scatter.4.cloned.1.call-start = ((), (), s32[]{:S(2)}) async-start(), calls=%async_computation.4 | async-start | bytes 5242880
Sparse Core Ops, SparseCore 0:
  33.7 44.1 all-gather.5
  154.5 130.5 all-reduce.2
  288.2 43.5 reduce-scatter.3
